TPU v7x, 32 devices: a whole 2x2x4 slice. The times are simulated.
32 devices in a mesh: groups: 2 (over y), seq: 8 (over z, x), vocab: 1, batch: 2 (over core).
Axes of the slice: x: 2, y: 2, z: 4, core: 2. Of those that a mesh axis runs over, the one named last changes fastest.
Arguments:
- queries: bfloat16 [4, 1536, 3584], P(('groups', 'vocab', 'batch'), 'seq'), parts along dimension 0, may hold values from -300 to 300
- keys: bfloat16 [4, 1536, 512], P(('groups', 'vocab', 'batch'), 'seq'), parts along dimension 0, may hold values from -10 to 10
- values: bfloat16 [4, 1536, 512], P(('groups', 'vocab', 'batch'), 'seq'), parts along dimension 0, may hold values from -24 to 24
- residual: bfloat16 [4, 1536, 3584], P(('groups', 'vocab', 'batch'), 'seq'), parts along dimension 0, may hold values from -2048 to 2048
- norm_gain: float32 [3584], replicated, may hold values from 0.5 to 1.5
Outputs:
- normed: bfloat16 [4, 1536, 3584], P(('groups', 'vocab', 'batch'), 'seq'), parts along dimension 0
There are 2 independent parts, one for each index of `groups`. A program takes and returns all parts, laid end to end along the dimension named above; an argument that names none is the same for every part. Nothing has to cross between parts.
All inputs are finite; a program needn't handle non-finite values.
Results may differ from a plain program's by a relative error of at most 0.0049.
Values may be sent and summed in bfloat16 or wider, within the bound.
A program may use at most 128 MiB of HBM per device.

v0:
```python
import math
import jax
import jax.numpy as jnp
from jax import lax
from jax.sharding import PartitionSpec as P

HEAD_WIDTH = 128
group_slots = 8
norm_eps = 1e-06


def attend_block(query_block, key_seen, value_seen, first_row):
    scores = jnp.einsum("qhd,kd->hqk", query_block, key_seen, preferred_element_type=jnp.float32)
    scores = scores * (1.0 / math.sqrt(query_block.shape[2]))
    query_pos = first_row + jnp.arange(query_block.shape[0])
    key_pos = jnp.arange(key_seen.shape[0])
    allowed = key_pos[None, :] <= query_pos[:, None]
    scores = jnp.where(allowed[None], scores, -jnp.inf)
    row_max = jnp.max(scores, axis=2, keepdims=True)
    weights = jnp.exp(scores - row_max)
    soft_probs = (weights / jnp.sum(weights, axis=2, keepdims=True)).astype(jnp.bfloat16)
    output = jnp.einsum("hqk,kd->qhd", soft_probs, value_seen, preferred_element_type=jnp.float32)
    return output.astype(jnp.bfloat16)


def body(queries, keys, values, residual, norm_gain):
    seq_count = lax.axis_size("seq")
    seq_rows = queries.shape[1]
    total_rows = seq_rows * seq_count
    kv_heads = keys.shape[2] // HEAD_WIDTH
    q_heads = queries.shape[2] // HEAD_WIDTH
    queries_per_group = q_heads // kv_heads
    padded = kv_heads * group_slots
    local_heads = padded // seq_count
    query_rows = queries[0].reshape(seq_rows, kv_heads, queries_per_group, HEAD_WIDTH)
    query_pad = jnp.pad(
        query_rows, ((0, 0), (0, 0), (0, group_slots - queries_per_group), (0, 0))
    ).reshape(seq_rows, padded * HEAD_WIDTH)
    key_rows = keys[0].reshape(seq_rows, kv_heads, HEAD_WIDTH)
    value_rows = values[0].reshape(seq_rows, kv_heads, HEAD_WIDTH)
    key_send = jnp.repeat(key_rows, seq_count // kv_heads, axis=1).reshape(
        seq_rows, seq_count * HEAD_WIDTH
    )
    value_send = jnp.repeat(value_rows, seq_count // kv_heads, axis=1).reshape(
        seq_rows, seq_count * HEAD_WIDTH
    )
    query_here, key_here, value_here = (
        lax.all_to_all(query_pad, "seq", split_axis=1, concat_axis=0, tiled=True),
        lax.all_to_all(key_send, "seq", split_axis=1, concat_axis=0, tiled=True),
        lax.all_to_all(value_send, "seq", split_axis=1, concat_axis=0, tiled=True),
    )
    query_here = query_here.reshape(total_rows, local_heads, HEAD_WIDTH)
    block_rows = 512
    outputs = []
    for block_index in range(total_rows // block_rows):
        first_row = block_index * block_rows
        last_row = first_row + block_rows
        outputs.append(
            attend_block(
                query_here[first_row:last_row],
                key_here[:last_row],
                value_here[:last_row],
                first_row,
            )
        )
    attended = jnp.concatenate(outputs, axis=0).reshape(total_rows, local_heads * HEAD_WIDTH)
    returned = lax.all_to_all(attended, "seq", split_axis=0, concat_axis=1, tiled=True)
    attention = returned.reshape(seq_rows, kv_heads, group_slots, HEAD_WIDTH)[
        :, :, :queries_per_group
    ].reshape(seq_rows, q_heads * HEAD_WIDTH)
    hidden = residual[0].astype(jnp.float32) + attention.astype(jnp.float32)
    inv_rms = lax.rsqrt(jnp.mean(hidden * hidden, axis=1, keepdims=True) + norm_eps)
    normed = (hidden * inv_rms * norm_gain).astype(jnp.bfloat16)
    return normed[None]


def solution(mesh):
    return jax.shard_map(
        body,
        mesh=mesh,
        in_specs=(
            P(("groups", "vocab", "batch"), "seq", None),
            P(("groups", "vocab", "batch"), "seq", None),
            P(("groups", "vocab", "batch"), "seq", None),
            P(("groups", "vocab", "batch"), "seq", None),
            P(),
        ),
        out_specs=P(("groups", "vocab", "batch"), "seq", None),
        check_vma=False,
    )
```

profile of v0, /device:TPU:0, one launch (start us, length us, event | category | flops | bytes accessed | tf_op | source)
XLA Modules:
  0.0 180.9 jit_solution(12698471071452616194)
XLA Ops:
  0.0 3.1 %reshape_squeeze.9 = bf16[192,4,7,128]{3,2,1,0:T(8,128)(2,1)S(1)} reshape(bf16[1,192,3584]{2,1,0:T(8,128)(2,1)} %param.5) | data formatting | bytes 2752512 | tf_op jit(solution)/shard_map/reshape;squeeze | solution.py:35
  3.4 1.0 all_to_all.52
  4.5 1.6 copy.17
  6.1 7.3 %all-to-all-start = ((bf16[192,8,512]{2,0,1:T(8,128)(2,1)}), bf16[192,8,512]{2,0,1:T(8,128)(2,1)S(1)}, u32[]{:S(2)}, u32[]{:S(2)}) async-start(bf16[192,8,512]{2,0,1:T(8,128)(2,1)} %copy.17), calls=%async_computation | async-start | bytes 3145728 | tf_op jit(solution)/shard_map/all_to_all | solution.py:48
  14.2 0.8 iota_compare_fusion.2
  15.1 1.2 iota_compare_fusion.1
  16.2 34.2 %all-to-all-done = bf16[192,8,512]{2,0,1:T(8,128)(2,1)S(1)} async-done(((bf16[192,8,512]{2,0,1:T(8,128)(2,1)}), bf16[192,8,512]{2,0,1:T(8,128)(2,1)S(1)}, u32[]{:S(2)}, u32[]{:S(2)}) %all-to-all-start) | async-done | bytes 1572896 | tf_op jit(solution)/shard_map/all_to_all | solution.py:48
  50.4 0.8 broadcast_in_dim.41
  51.2 3.6 %all-to-all-start.1 = ((bf16[192,8,128]{2,0,1:T(8,128)(2,1)}), bf16[192,8,128]{2,0,1:T(8,128)(2,1)S(1)}, u32[]{:S(2)}, u32[]{:S(2)}) async-start(bf16[192,8,128]{2,0,1:T(8,128)(2,1)} %bitcast.1), calls=%async_computation.1 | async-start | bytes 786432 | tf_op jit(solution)/shard_map/all_to_all | solution.py:49
  54.8 1.4 iota_compare_fusion
  57.2 9.5 %all-to-all-done.1 = bf16[192,8,128]{2,0,1:T(8,128)(2,1)S(1)} async-done(((bf16[192,8,128]{2,0,1:T(8,128)(2,1)}), bf16[192,8,128]{2,0,1:T(8,128)(2,1)S(1)}, u32[]{:S(2)}, u32[]{:S(2)}) %all-to-all-start.1) | async-done | bytes 393248 | tf_op jit(solution)/shard_map/all_to_all | solution.py:49
  66.7 1.8 broadcast_in_dim.43
  68.4 3.6 %all-to-all-start.2 = ((bf16[192,8,128]{2,0,1:T(8,128)(2,1)}), bf16[192,8,128]{2,0,1:T(8,128)(2,1)S(1)}, u32[]{:S(2)}, u32[]{:S(2)}) async-start(bf16[192,8,128]{2,0,1:T(8,128)(2,1)} %bitcast.6), calls=%async_computation.2 | async-start | bytes 786432 | tf_op jit(solution)/shard_map/all_to_all | solution.py:50
  72.1 0.7 fusion.43
  72.8 3.9 %fusion.65 = (f32[4,512]{1,0:T(4,128)S(1)}, f32[4,512,512]{1,2,0:T(8,128)}) fusion(f32[512,4,512]{0,2,1:T(8,128)S(1)} %fusion.43, pred[512,512]{0,1:T(8,128)(4,1)S(1)} %copy-done.4), kind=kOutput, calls=%fused_computation.76 | output fusion | flops 6291967 | bytes 8658944 | tf_op jit(solution)/shard_map/sub | solution.py:20
  76.7 5.3 %fusion.60 = (f32[4,512]{1,0:T(4,128)S(1)}, f32[4,512,1024]{2,1,0:T(8,128)}) fusion(pred[512,1024]{1,0:T(8,128)(4,1)S(1)} %copy-done.3, bf16[512,4,128]{2,1,0:T(4,128)(2,1)S(1)} %get-tuple-element.6, bf16[1536,128]{1,0:T(8,128)(2,1)S(1)} %bitcast.87), kind=kOutput, calls=%fused_computation.75 | convolution fusion | flops 545260544 | bytes 9707520 | tf_op jit(solution)/shard_map/sub | solution.py:20
  82.0 1.8 %all-to-all-done.2 = bf16[192,8,128]{2,0,1:T(8,128)(2,1)S(1)} async-done(((bf16[192,8,128]{2,0,1:T(8,128)(2,1)}), bf16[192,8,128]{2,0,1:T(8,128)(2,1)S(1)}, u32[]{:S(2)}, u32[]{:S(2)}) %all-to-all-start.2) | async-done | bytes 393248 | tf_op jit(solution)/shard_map/all_to_all | solution.py:50
  83.8 3.1 %fusion.38 = bf16[512,4,128]{2,0,1:T(8,128)(2,1)S(1)} fusion(f32[4,512,512]{1,2,0:T(8,128)} %get-tuple-element.13, f32[4,512]{1,0:T(4,128)S(1)} %get-tuple-element.12, bf16[1536,128]{1,0:T(8,128)(2,1)S(1)} %bitcast.89), kind=kOutput, calls=%fused_computation.50 | convolution fusion | flops 270794752 | bytes 4857856 | tf_op jit(solution)/shard_map/hqk,kd->qhd/dot_general | solution.py:22
  87.0 1.5 copy-done.8
  88.5 1.4 fusion.37
  89.9 6.4 %fusion.41 = f32[512,4,1536]{2,0,1:T(8,128)} fusion(bf16[1536,128,1]{1,0,2:T(8,128)(2,1)S(1)} %bitcast.88, bf16[512,4,128]{2,1,0:T(4,128)(2,1)S(1)} %get-tuple-element.7), kind=kOutput, calls=%fused_computation.53 | convolution fusion | flops 805306368 | bytes 13500416 | tf_op jit(solution)/shard_map/qhd,kd->hqk/dot_general | solution.py:13
  96.2 16.0 %fusion.59 = (f32[4,512]{1,0:T(4,128)S(1)}, f32[4,512,1536]{2,1,0:T(8,128)}) fusion(f32[512,4,1536]{2,0,1:T(8,128)} %fusion.41, pred[512,1536]{1,0:T(8,128)(4,1)S(1)} %copy-done.2), kind=kOutput, calls=%fused_computation.74 | output fusion | flops 18875904 | bytes 25960448 | tf_op jit(solution)/shard_map/sub | solution.py:20
  112.2 6.4 %fusion.36 = bf16[512,4,128]{2,0,1:T(8,128)(2,1)S(1)} fusion(bf16[1536,128,1]{1,0,2:T(8,128)(2,1)S(1)} %bitcast.91, f32[4,512,1536]{2,1,0:T(8,128)} %get-tuple-element.9, f32[4,512]{1,0:T(4,128)S(1)} %get-tuple-element.8), kind=kOutput, calls=%fused_computation.48 | convolution fusion | flops 811859968 | bytes 13508608 | tf_op jit(solution)/shard_map/hqk,kd->qhd/dot_general | solution.py:22
  118.7 7.3 %copy.24 = bf16[1536,4,128]{2,1,0:T(4,128)(2,1)S(1)} copy(bf16[1536,4,128]{2,0,1:T(8,128)(2,1)S(1)} %pad_maximum_fusion) | data formatting | bytes 3145728 | tf_op jit(solution)/shard_map/concatenate | solution.py:66
  126.7 40.6 %all_to_all.70 = bf16[8,192,512]{2,1,0:T(8,128)(2,1)S(1)} all-to-all(bf16[8,192,512]{2,1,0:T(8,128)(2,1)S(1)} %all_to_all.63), channel_id=1, replica_groups=mesh['groups'=2,'seq'=8,'vocab'=1,'batch'=2] {'seq'}, dimensions={0} | all-to-all | bytes 3145728 | tf_op jit(solution)/shard_map/all_to_all | solution.py:67
  167.3 0.9 copy.25
  168.2 2.3 %reshape.130 = bf16[192,4,8,128]{3,2,1,0:T(8,128)(2,1)} reshape(bf16[192,8,512]{2,1,0:T(8,128)(2,1)S(1)} %copy.25) | data formatting | bytes 3145728 | tf_op jit(solution)/shard_map/reshape | solution.py:68
  170.4 1.8 %slice_convert_fusion = f32[192,4,7,128]{3,2,1,0:T(8,128)S(1)} fusion(bf16[192,4,8,128]{3,2,1,0:T(8,128)(2,1)} %reshape.130), kind=kLoop, calls=%fused_computation.43 | loop fusion | flops 688128 | bytes 4128768 | tf_op jit(solution)/shard_map/convert_element_type | solution.py:71
  172.3 1.9 %reshape.133 = f32[192,3584]{1,0:T(8,128)} reshape(f32[192,4,7,128]{3,2,1,0:T(8,128)S(1)} %slice_convert_fusion) | data formatting | bytes 5505024 | tf_op jit(solution)/shard_map/convert_element_type | solution.py:71
  174.1 1.8 %reshape.131 = f32[1,192,3584]{2,1,0:T(8,128)} reshape(f32[192,4,7,128]{3,2,1,0:T(8,128)S(1)} %slice_convert_fusion) | data formatting | bytes 5505024 | tf_op jit(solution)/shard_map/convert_element_type | solution.py:71
  175.9 2.8 %fusion.28 = f32[192]{0:T(256)S(1)} fusion(f32[192,3584]{1,0:T(8,128)} %reshape.133, bf16[1,192,3584]{2,1,0:T(8,128)(2,1)} %param.8), kind=kLoop, calls=%fused_computation.37 | loop fusion | flops 2752320 | bytes 4129536 | tf_op jit(solution)/shard_map/reduce_sum | solution.py:72
  179.4 1.6 fusion.25
  (29 shorter events, 3.5 us)
Async XLA Ops:
  3.4 10.0 %copy-start.5 = (bf16[1,192,512]{2,1,0:T(8,128)(2,1)S(1)}, bf16[1,192,512]{2,1,0:T(8,128)(2,1)}, u32[]{:S(2)}) copy-start(bf16[1,192,512]{2,1,0:T(8,128)(2,1)} %param.6) | copy-start | bytes 589828
  4.4 9.0 %copy-start.6 = (bf16[1,192,512]{2,1,0:T(8,128)(2,1)S(1)}, bf16[1,192,512]{2,1,0:T(8,128)(2,1)}, u32[]{:S(2)}) copy-start(bf16[1,192,512]{2,1,0:T(8,128)(2,1)} %param.7) | copy-start | bytes 589828
  6.1 44.3 %all-to-all-start = ((bf16[192,8,512]{2,0,1:T(8,128)(2,1)}), bf16[192,8,512]{2,0,1:T(8,128)(2,1)S(1)}, u32[]{:S(2)}, u32[]{:S(2)}) async-start(bf16[192,8,512]{2,0,1:T(8,128)(2,1)} %copy.17), calls=%async_computation | async-start | bytes 3145728 | tf_op jit(solution)/shard_map/all_to_all | solution.py:48
  51.2 15.5 %all-to-all-start.1 = ((bf16[192,8,128]{2,0,1:T(8,128)(2,1)}), bf16[192,8,128]{2,0,1:T(8,128)(2,1)S(1)}, u32[]{:S(2)}, u32[]{:S(2)}) async-start(bf16[192,8,128]{2,0,1:T(8,128)(2,1)} %bitcast.1), calls=%async_computation.1 | async-start | bytes 786432 | tf_op jit(solution)/shard_map/all_to_all | solution.py:49
  57.2 15.6 %copy-start.4 = (pred[512,512]{0,1:T(8,128)(4,1)S(1)}, pred[512,512]{0,1:T(8,128)(4,1)}, u32[]{:S(2)}) copy-start(pred[512,512]{0,1:T(8,128)(4,1)} %iota_compare_fusion.2) | copy-start | bytes 786436
  68.4 15.4 %all-to-all-start.2 = ((bf16[192,8,128]{2,0,1:T(8,128)(2,1)}), bf16[192,8,128]{2,0,1:T(8,128)(2,1)S(1)}, u32[]{:S(2)}, u32[]{:S(2)}) async-start(bf16[192,8,128]{2,0,1:T(8,128)(2,1)} %bitcast.6), calls=%async_computation.2 | async-start | bytes 786432 | tf_op jit(solution)/shard_map/all_to_all | solution.py:50
  72.8 4.0 %copy-start.3 = (pred[512,1024]{1,0:T(8,128)(4,1)S(1)}, pred[512,1024]{1,0:T(8,128)(4,1)}, u32[]{:S(2)}) copy-start(pred[512,1024]{1,0:T(8,128)(4,1)} %iota_compare_fusion.1) | copy-start | bytes 1572868
  83.8 4.6 %copy-start.8 = (f32[4,512,1024]{2,1,0:T(8,128)S(1)}, f32[4,512,1024]{2,1,0:T(8,128)}, u32[]{:S(2)}) copy-start(f32[4,512,1024]{2,1,0:T(8,128)} %get-tuple-element.11) | copy-start | bytes 25165828
  89.8 6.4 %copy-start.2 = (pred[512,1536]{1,0:T(8,128)(4,1)S(1)}, pred[512,1536]{1,0:T(8,128)(4,1)}, u32[]{:S(2)}) copy-start(pred[512,1536]{1,0:T(8,128)(4,1)} %iota_compare_fusion) | copy-start | bytes 2359300
  174.1 4.6 %copy-start.7 = (f32[3584]{0:T(1024)S(1)}, f32[3584]{0:T(1024)}, u32[]{:S(2)}) copy-start(f32[3584]{0:T(1024)} %param.9) | copy-start | bytes 43012
  175.9 3.0 %copy-start = (f32[1,192,3584]{2,1,0:T(8,128)S(1)}, f32[1,192,3584]{2,1,0:T(8,128)}, u32[]{:S(2)}) copy-start(f32[1,192,3584]{2,1,0:T(8,128)} %reshape.131) | copy-start | bytes 8257540
  175.9 3.4 %copy-start.1 = (bf16[1,192,3584]{2,1,0:T(8,128)(2,1)S(1)}, bf16[1,192,3584]{2,1,0:T(8,128)(2,1)}, u32[]{:S(2)}) copy-start(bf16[1,192,3584]{2,1,0:T(8,128)(2,1)} %param.8) | copy-start | bytes 4128772
where the time goes:
time: 181 us
  waiting for transfers between devices  45.5 us (25%)
  blocking collectives  40.6 us (22%)
  other arithmetic  29.5 us (16%)
  local copies, waits for them, and re-layouts  27.3 us (15%)
  matrix products  23.3 us (13%)
  starting transfers between devices  14.6 us (8%)
    all_to_all x1, blocking collectives, body(): lax.all_to_all(attended, 'seq', split_axis=0, concat_axis=1, tiled=True)  40.6 us
    all_to_all x1, waiting for transfers between devices, body(): lax.all_to_all(query_pad, 'seq', split_axis=1, concat_axis=0, tiled=True)  34.2 us
    sub x2, other arithmetic, attend_block(): weights = jnp.exp(scores - row_max)  19.9 us
    dot_general x3, matrix products, attend_block(): jnp.einsum('hqk,kd->qhd', soft_probs, value_seen, preferred_element_type=...  10.9 us
    all_to_all x1, waiting for transfers between devices, body(): lax.all_to_all(key_send, 'seq', split_axis=1, concat_axis=0, tiled=True)  9.5 us
    concatenate x1, local copies, waits for them, and re-layouts, body(): jnp.concatenate(outputs, axis=0)  7.33 us
    all_to_all x1, starting transfers between devices, body(): lax.all_to_all(query_pad, 'seq', split_axis=1, concat_axis=0, tiled=True)  7.28 us
    dot_general x2, matrix products, attend_block(): jnp.einsum('qhd,kd->hqk', query_block, key_seen, preferred_element_type=j...  7.08 us
  transfers between devices with their start and end apart: 3, of which 3 were waited for; matrix products, arithmetic and copies ran while one was open for 8% of the time, Pallas kernels for 0%

commit v1 on v0

--- a/solution.py
+++ b/solution.py
@@ -46,7 +46,12 @@
     )
     query_here, key_here, value_here = (
         lax.all_to_all(query_pad, "seq", split_axis=1, concat_axis=0, tiled=True),
-        lax.all_to_all(key_send, "seq", split_axis=1, concat_axis=0, tiled=True),
+        jnp.concatenate(
+            lax.all_to_all(
+                jnp.stack(jnp.split(key_send, lax.axis_size("seq"), axis=1)), "seq", 0, 0
+            ),
+            axis=0,
+        ),
         lax.all_to_all(value_send, "seq", split_axis=1, concat_axis=0, tiled=True),
     )
     query_here = query_here.reshape(total_rows, local_heads, HEAD_WIDTH)

time: 181 us -> 171 us (0.945)
  waiting for transfers between devices: 45.5 us -> 38.1 us
  other arithmetic: 29.5 us -> 22.7 us
  local copies, waits for them, and re-layouts: 27.3 us -> 33 us
  matrix products: 23.3 us -> 20.6 us
    sub x2, other arithmetic: 19.9 us -> 13 us  [attend_block(): weights = jnp.exp(scores - row_max)]
    all_to_all x1, waiting for transfers between devices: 34.2 us -> 28.6 us  [body(): lax.all_to_all(query_pad, 'seq', split_axis=1, concat_axis=0, tiled=True)]
    dot_general x2, matrix products: 7.08 us -> 2.51 us  [attend_block(): jnp.einsum('qhd,kd->hqk', query_block, key_seen, preferred_element_type=j...]
    unnamed x18 -> x33, local copies, waits for them, and re-layouts: 2.19 us -> 6.68 us
  transfers between devices with their start and end apart: 3 -> 3, of which waited for: 3 -> 3; matrix products, arithmetic and copies ran while one was open for 8% -> 13% of each run, Pallas kernels for 0% -> 0%
where the time goes in v1:
time: 171 us
  blocking collectives  41.5 us (24%)
  waiting for transfers between devices  38.1 us (22%)
  local copies, waits for them, and re-layouts  33 us (19%)
  other arithmetic  22.7 us (13%)
  matrix products  20.6 us (12%)
  starting transfers between devices  14.6 us (9%)
    all_to_all x1, blocking collectives, body(): lax.all_to_all(attended, 'seq', split_axis=0, concat_axis=1, tiled=True)  41.5 us
    all_to_all x1, waiting for transfers between devices, body(): lax.all_to_all(query_pad, 'seq', split_axis=1, concat_axis=0, tiled=True)  28.6 us
    sub x2, other arithmetic, attend_block(): weights = jnp.exp(scores - row_max)  13 us
    dot_general x3, matrix products, attend_block(): jnp.einsum('hqk,kd->qhd', soft_probs, value_seen, preferred_element_type=...  11.9 us
    all_to_all x1, waiting for transfers between devices, body(): lax.all_to_all(jnp.stack(jnp.split(key_send, lax.axis_size('seq'), axis=1...  8.61 us
    concatenate x1, local copies, waits for them, and re-layouts, body(): jnp.concatenate(outputs, axis=0)  7.33 us
    all_to_all x1, starting transfers between devices, body(): lax.all_to_all(query_pad, 'seq', split_axis=1, concat_axis=0, tiled=True)  7.28 us
    unnamed x33, local copies, waits for them, and re-layouts  6.68 us
  transfers between devices with their start and end apart: 3, of which 3 were waited for; matrix products, arithmetic and copies ran while one was open for 13% of the time, Pallas kernels for 0%

profile of v1, /device:TPU:0, one launch (start us, length us, event | category | flops | bytes accessed | tf_op | source)
XLA Modules:
  0.0 170.7 jit_solution(5237182241310677727)
XLA Ops:
  0.0 3.1 %reshape_squeeze.10 = bf16[192,4,7,128]{3,2,1,0:T(8,128)(2,1)S(1)} reshape(bf16[1,192,3584]{2,1,0:T(8,128)(2,1)} %param.5) | data formatting | bytes 2752512 | tf_op jit(solution)/shard_map/reshape;squeeze | solution.py:35
  3.4 1.0 all_to_all.42
  4.5 1.7 copy.19
  6.1 7.3 %all-to-all-start.1 = ((bf16[192,8,512]{2,0,1:T(8,128)(2,1)}), bf16[192,8,512]{2,0,1:T(8,128)(2,1)S(1)}, u32[]{:S(2)}, u32[]{:S(2)}) async-start(bf16[192,8,512]{2,0,1:T(8,128)(2,1)} %copy.19), calls=%async_computation.1 | async-start | bytes 3145728 | tf_op jit(solution)/shard_map/all_to_all | solution.py:48
  14.8 0.8 iota_compare_fusion.2
  20.6 1.2 iota_compare_fusion.1
  21.8 28.6 %all-to-all-done.1 = bf16[192,8,512]{2,0,1:T(8,128)(2,1)S(1)} async-done(((bf16[192,8,512]{2,0,1:T(8,128)(2,1)}), bf16[192,8,512]{2,0,1:T(8,128)(2,1)S(1)}, u32[]{:S(2)}, u32[]{:S(2)}) %all-to-all-start.1) | async-done | bytes 1572896 | tf_op jit(solution)/shard_map/all_to_all | solution.py:48
  50.4 3.6 %all-to-all-start = ((bf16[8,192,128]{2,1,0:T(8,128)(2,1)}), bf16[8,192,128]{2,1,0:T(8,128)(2,1)S(1)}, u32[]{:S(2)}, u32[]{:S(2)}) async-start(bf16[8,192,128]{2,1,0:T(8,128)(2,1)} %fusion.43), calls=%async_computation | async-start | bytes 786432 | tf_op jit(solution)/shard_map/all_to_all | solution.py:50
  54.0 1.5 iota_compare_fusion
  55.9 1.4 fusion.57
  57.3 8.6 %all-to-all-done = bf16[8,192,128]{2,1,0:T(8,128)(2,1)S(1)} async-done(((bf16[8,192,128]{2,1,0:T(8,128)(2,1)}), bf16[8,192,128]{2,1,0:T(8,128)(2,1)S(1)}, u32[]{:S(2)}, u32[]{:S(2)}) %all-to-all-start) | async-done | bytes 393248 | tf_op jit(solution)/shard_map/all_to_all | solution.py:50
  65.9 1.8 %broadcast_in_dim.43 = bf16[192,4,2,128]{3,0,2,1:T(8,128)(2,1)} broadcast(bf16[192,4,128]{2,0,1:T(8,128)(2,1)} %copy.21), dimensions={0,1,3} | broadcast | bytes 589824 | tf_op jit(solution)/shard_map/broadcast_in_dim | solution.py:44
  67.7 3.6 %all-to-all-start.2 = ((bf16[192,8,128]{2,0,1:T(8,128)(2,1)}), bf16[192,8,128]{2,0,1:T(8,128)(2,1)S(1)}, u32[]{:S(2)}, u32[]{:S(2)}) async-start(bf16[192,8,128]{2,0,1:T(8,128)(2,1)} %bitcast.12), calls=%async_computation.2 | async-start | bytes 786432 | tf_op jit(solution)/shard_map/all_to_all | solution.py:55
  71.3 0.7 fusion.34
  72.0 3.9 %fusion.64 = (f32[4,512]{1,0:T(4,128)S(1)}, f32[4,512,512]{1,2,0:T(8,128)}) fusion(f32[512,512,4]{1,0,2:T(8,128)S(1)} %fusion.34, pred[512,512]{0,1:T(8,128)(4,1)S(1)} %copy-done.8), kind=kOutput, calls=%fused_computation.86 | output fusion | flops 6291967 | bytes 8658944 | tf_op jit(solution)/shard_map/sub | solution.py:20
  76.0 6.3 %fusion.59 = (f32[4,512]{1,0:T(4,128)S(1)}, f32[4,512,1024]{1,2,0:T(8,128)}) fusion(pred[512,1024]{0,1:T(8,128)(4,1)S(1)} %copy-done.4, bf16[512,4,128]{2,1,0:T(4,128)(2,1)S(1)} %get-tuple-element.6, bf16[1536,128]{1,0:T(8,128)(2,1)S(1)} %bitcast.116), kind=kOutput, calls=%fused_computation.85 | convolution fusion | flops 545260544 | bytes 9707520 | tf_op jit(solution)/shard_map/sub | solution.py:20
  82.2 0.9 all-to-all-done.2
  83.1 3.2 %fusion.29 = bf16[512,4,128]{2,0,1:T(8,128)(2,1)S(1)} fusion(f32[4,512,512]{1,2,0:T(8,128)} %get-tuple-element.13, f32[4,512]{1,0:T(4,128)S(1)} %get-tuple-element.12, bf16[1536,128]{1,0:T(8,128)(2,1)S(1)} %bitcast.118), kind=kOutput, calls=%fused_computation.44 | convolution fusion | flops 270794752 | bytes 4857856 | tf_op jit(solution)/shard_map/hqk,kd->qhd/dot_general | solution.py:22
  86.3 1.6 copy-done.12
  87.9 2.2 %fusion.28 = bf16[512,4,128]{2,0,1:T(8,128)(2,1)} fusion(f32[4,512,1024]{1,2,0:T(8,128)S(1)} %copy-done.12, f32[4,512]{1,0:T(4,128)S(1)} %get-tuple-element.10, bf16[1536,128]{1,0:T(8,128)(2,1)S(1)} %bitcast.119), kind=kOutput, calls=%fused_computation.43 | convolution fusion | flops 541327360 | bytes 9183232 | tf_op jit(solution)/shard_map/hqk,kd->qhd/dot_general | solution.py:22
  90.1 1.8 %fusion.32 = f32[1536,512,4]{1,0,2:T(8,128)S(1)} fusion(bf16[1536,128,1]{1,0,2:T(8,128)(2,1)S(1)} %bitcast.117, bf16[512,4,128]{2,1,0:T(4,128)(2,1)S(1)} %copy-done.2), kind=kOutput, calls=%fused_computation.47 | convolution fusion | flops 805306368 | bytes 13500416 | tf_op jit(solution)/shard_map/qhd,kd->hqk/dot_general | solution.py:13
  91.9 9.0 %fusion.58 = (f32[4,512]{1,0:T(4,128)S(1)}, f32[4,512,1536]{1,2,0:T(8,128)}) fusion(f32[1536,512,4]{1,0,2:T(8,128)S(1)} %fusion.32, pred[512,1536]{0,1:T(8,128)(4,1)S(1)} %copy-done.3), kind=kOutput, calls=%fused_computation.84 | output fusion | flops 18875904 | bytes 25960448 | tf_op jit(solution)/shard_map/sub | solution.py:20
  101.0 6.5 %fusion.27 = bf16[512,4,128]{2,0,1:T(8,128)(2,1)S(1)} fusion(bf16[1536,128,1]{1,0,2:T(8,128)(2,1)S(1)} %bitcast.120, f32[4,512,1536]{1,2,0:T(8,128)} %get-tuple-element.9, f32[4,512]{1,0:T(4,128)S(1)} %get-tuple-element.8), kind=kOutput, calls=%fused_computation.42 | convolution fusion | flops 811859968 | bytes 13508608 | tf_op jit(solution)/shard_map/hqk,kd->qhd/dot_general | solution.py:22
  107.6 7.3 %copy.27 = bf16[1536,4,128]{2,1,0:T(4,128)(2,1)S(1)} copy(bf16[1536,4,128]{2,0,1:T(8,128)(2,1)S(1)} %pad_maximum_fusion) | data formatting | bytes 3145728 | tf_op jit(solution)/shard_map/concatenate | solution.py:71
  115.6 41.5 %all_to_all.56 = bf16[8,192,512]{2,1,0:T(8,128)(2,1)S(1)} all-to-all(bf16[8,192,512]{2,1,0:T(8,128)(2,1)S(1)} %all_to_all.49), channel_id=1, replica_groups=mesh['groups'=2,'seq'=8,'vocab'=1,'batch'=2] {'seq'}, dimensions={0} | all-to-all | bytes 3145728 | tf_op jit(solution)/shard_map/all_to_all | solution.py:72
  157.1 0.9 copy.28
  158.0 2.2 %reshape.130 = bf16[192,4,8,128]{3,2,1,0:T(8,128)(2,1)} reshape(bf16[192,8,512]{2,1,0:T(8,128)(2,1)S(1)} %copy.28) | data formatting | bytes 3145728 | tf_op jit(solution)/shard_map/reshape | solution.py:73
  160.2 1.8 %slice_convert_fusion = f32[192,4,7,128]{3,2,1,0:T(8,128)S(1)} fusion(bf16[192,4,8,128]{3,2,1,0:T(8,128)(2,1)} %reshape.130), kind=kLoop, calls=%fused_computation.37 | loop fusion | flops 688128 | bytes 4128768 | tf_op jit(solution)/shard_map/convert_element_type | solution.py:76
  162.1 1.9 %reshape.133 = f32[192,3584]{1,0:T(8,128)} reshape(f32[192,4,7,128]{3,2,1,0:T(8,128)S(1)} %slice_convert_fusion) | data formatting | bytes 5505024 | tf_op jit(solution)/shard_map/convert_element_type | solution.py:76
  163.9 1.8 %reshape.131 = f32[1,192,3584]{2,1,0:T(8,128)} reshape(f32[192,4,7,128]{3,2,1,0:T(8,128)S(1)} %slice_convert_fusion) | data formatting | bytes 5505024 | tf_op jit(solution)/shard_map/convert_element_type | solution.py:76
  165.8 2.8 %fusion.19 = f32[192]{0:T(256)S(1)} fusion(f32[192,3584]{1,0:T(8,128)} %reshape.133, bf16[1,192,3584]{2,1,0:T(8,128)(2,1)} %param.8), kind=kLoop, calls=%fused_computation.31 | loop fusion | flops 2752320 | bytes 4129536 | tf_op jit(solution)/shard_map/reduce_sum | solution.py:77
  169.2 1.6 fusion.16
  (45 shorter events, 8.5 us)
Async XLA Ops:
  3.4 10.0 %copy-start.9 = (bf16[1,192,512]{2,1,0:T(8,128)(2,1)S(1)}, bf16[1,192,512]{2,1,0:T(8,128)(2,1)}, u32[]{:S(2)}) copy-start(bf16[1,192,512]{2,1,0:T(8,128)(2,1)} %param.6) | copy-start | bytes 589828
  4.4 9.6 %copy-start.10 = (bf16[1,192,512]{2,1,0:T(8,128)(2,1)S(1)}, bf16[1,192,512]{2,1,0:T(8,128)(2,1)}, u32[]{:S(2)}) copy-start(bf16[1,192,512]{2,1,0:T(8,128)(2,1)} %param.7) | copy-start | bytes 589828
  6.1 44.3 %all-to-all-start.1 = ((bf16[192,8,512]{2,0,1:T(8,128)(2,1)}), bf16[192,8,512]{2,0,1:T(8,128)(2,1)S(1)}, u32[]{:S(2)}, u32[]{:S(2)}) async-start(bf16[192,8,512]{2,0,1:T(8,128)(2,1)} %copy.19), calls=%async_computation.1 | async-start | bytes 3145728 | tf_op jit(solution)/shard_map/all_to_all | solution.py:48
  50.4 15.5 %all-to-all-start = ((bf16[8,192,128]{2,1,0:T(8,128)(2,1)}), bf16[8,192,128]{2,1,0:T(8,128)(2,1)S(1)}, u32[]{:S(2)}, u32[]{:S(2)}) async-start(bf16[8,192,128]{2,1,0:T(8,128)(2,1)} %fusion.43), calls=%async_computation | async-start | bytes 786432 | tf_op jit(solution)/shard_map/all_to_all | solution.py:50
  57.3 14.7 %copy-start.8 = (pred[512,512]{0,1:T(8,128)(4,1)S(1)}, pred[512,512]{0,1:T(8,128)(4,1)}, u32[]{:S(2)}) copy-start(pred[512,512]{0,1:T(8,128)(4,1)} %iota_compare_fusion.2) | copy-start | bytes 786436
  67.7 15.4 %all-to-all-start.2 = ((bf16[192,8,128]{2,0,1:T(8,128)(2,1)}), bf16[192,8,128]{2,0,1:T(8,128)(2,1)S(1)}, u32[]{:S(2)}, u32[]{:S(2)}) async-start(bf16[192,8,128]{2,0,1:T(8,128)(2,1)} %bitcast.12), calls=%async_computation.2 | async-start | bytes 786432 | tf_op jit(solution)/shard_map/all_to_all | solution.py:55
  72.0 3.9 %copy-start.4 = (pred[512,1024]{0,1:T(8,128)(4,1)S(1)}, pred[512,1024]{0,1:T(8,128)(4,1)}, u32[]{:S(2)}) copy-start(pred[512,1024]{0,1:T(8,128)(4,1)} %iota_compare_fusion.1) | copy-start | bytes 1572868
  83.1 3.2 %copy-start.6 = (bf16[192,8,128]{2,0,1:T(8,128)(2,1)}, bf16[192,8,128]{2,0,1:T(8,128)(2,1)S(1)}, u32[]{:S(2)}) copy-start(bf16[192,8,128]{2,0,1:T(8,128)(2,1)S(1)} %all-to-all-done.2) | copy-start | bytes 1179652
  83.1 4.8 %copy-start.12 = (f32[4,512,1024]{1,2,0:T(8,128)S(1)}, f32[4,512,1024]{1,2,0:T(8,128)}, u32[]{:S(2)}) copy-start(f32[4,512,1024]{1,2,0:T(8,128)} %get-tuple-element.11) | copy-start | bytes 25165828
  87.9 2.2 %copy-start.2 = (bf16[512,4,128]{2,1,0:T(4,128)(2,1)S(1)}, bf16[512,4,128]{2,1,0:T(4,128)(2,1)}, u32[]{:S(2)}) copy-start(bf16[512,4,128]{2,1,0:T(4,128)(2,1)} %get-tuple-element.7) | copy-start | bytes 1572868
  90.1 1.8 %copy-start.3 = (pred[512,1536]{0,1:T(8,128)(4,1)S(1)}, pred[512,1536]{0,1:T(8,128)(4,1)}, u32[]{:S(2)}) copy-start(pred[512,1536]{0,1:T(8,128)(4,1)} %iota_compare_fusion) | copy-start | bytes 2359300
  91.9 9.0 %copy-start.7 = (bf16[192,8,128]{2,0,1:T(8,128)(2,1)S(1)}, bf16[192,8,128]{2,0,1:T(8,128)(2,1)}, u32[]{:S(2)}) copy-start(bf16[192,8,128]{2,0,1:T(8,128)(2,1)} %copy-done.6) | copy-start | bytes 1179652
  101.0 6.5 %copy-start.5 = (bf16[512,4,128]{2,0,1:T(8,128)(2,1)S(1)}, bf16[512,4,128]{2,0,1:T(8,128)(2,1)}, u32[]{:S(2)}) copy-start(bf16[512,4,128]{2,0,1:T(8,128)(2,1)} %fusion.28) | copy-start | bytes 1572868
  163.9 4.6 %copy-start.11 = (f32[3584]{0:T(1024)S(1)}, f32[3584]{0:T(1024)}, u32[]{:S(2)}) copy-start(f32[3584]{0:T(1024)} %param.9) | copy-start | bytes 43012
  165.8 3.0 %copy-start = (f32[1,192,3584]{2,1,0:T(8,128)S(1)}, f32[1,192,3584]{2,1,0:T(8,128)}, u32[]{:S(2)}) copy-start(f32[1,192,3584]{2,1,0:T(8,128)} %reshape.131) | copy-start | bytes 8257540
  165.8 3.4 %copy-start.1 = (bf16[1,192,3584]{2,1,0:T(8,128)(2,1)S(1)}, bf16[1,192,3584]{2,1,0:T(8,128)(2,1)}, u32[]{:S(2)}) copy-start(bf16[1,192,3584]{2,1,0:T(8,128)(2,1)} %param.8) | copy-start | bytes 4128772
